TPU v7x, 32 devices: a whole 2x2x4 slice. The times are simulated.
32 devices in a mesh: dp: 4 (over y, core), seq: 2 (over x), expert: 4 (over z).
Axes of the slice: x: 2, y: 2, z: 4, core: 2. Of those that a mesh axis runs over, the one named last changes fastest.
Arguments:
- queries: bfloat16 [16, 256, 2560], P(('dp', 'expert'), 'seq'), may hold values from -100 to 100
- key_rows: bfloat16 [16, 256, 512], P(('dp', 'expert'), 'seq'), may hold values from -5 to 5
- value_entries: bfloat16 [16, 256, 512], P(('dp', 'expert'), 'seq'), may hold values from -6 to 6
- features: bfloat16 [4096, 2560], P(('dp', 'seq', 'expert')), may hold values from -0.29882812 to 0.29882812
- router_score: float32 [4096], P(('dp', 'seq', 'expert')), may hold values from -8 to 8
- expert_index: int32 [4096], P(('dp', 'seq', 'expert')), may hold values from 0 to 31, as said below
- slot_index: int32 [4096], P(('dp', 'seq', 'expert')), may hold values from 0 to 35, as said below
- expert_grad: bfloat16 [4608, 2560], P(('dp', 'seq', 'expert')), may hold values from -12 to 12
Outputs:
- attention: bfloat16 [16, 256, 2560], P(('dp', 'expert'), 'seq')
- input_grad: bfloat16 [4096, 2560], P(('dp', 'seq', 'expert'))
- score_grad: float32 [4096], P(('dp', 'seq', 'expert'))
- router_grad: float32 [32, 2560], P('expert', ('dp', 'seq'))
Inputs may be any that keep to these rules, and one draw needn't show every extreme that they name: Among the 128 tokens of one device (aligned blocks, devices in the order dp, seq, expert), at most 36 have one value of expert_index // 8; in every draw some value takes exactly 36 tokens in every block. Tokens of one block with the same expert_index // 8 have different slot_index.
All inputs are finite; a program needn't handle non-finite values.
Results may differ from a plain program's by a relative error of at most 0.0046.
Values may be sent and summed in bfloat16 or wider, within the bound.
No kernel may reach another device: no remote copies, remote signals or barrier semaphores. Data moves between devices by JAX's collectives and lax.ppermute only.
A program may use at most 64 MiB of HBM per device.

v0:
```python
import math
import jax
import jax.numpy as jnp
from jax import lax
from jax.sharding import PartitionSpec as P

HEAD_SIZE = 128
EXP_DEV = 8


def attend_rows(query_part, key_part, value_part, query_start):
    row_count = query_part.shape[0]
    key_count = key_part.shape[0]
    key_heads = key_part.shape[1] // HEAD_SIZE
    group_width = query_part.shape[1] // (key_heads * HEAD_SIZE)
    query_tiles = query_part.reshape(row_count, key_heads, group_width, HEAD_SIZE)
    key_tiles = key_part.reshape(key_count, key_heads, HEAD_SIZE)
    value_tiles = value_part.reshape(key_count, key_heads, HEAD_SIZE)
    scores = jnp.einsum(
        "qkgd,pkd->kgqp", query_tiles, key_tiles, preferred_element_type=jnp.float32
    ) * (1.0 / math.sqrt(HEAD_SIZE))
    query_pos = query_start + lax.broadcasted_iota(jnp.int32, (row_count, key_count), 0)
    key_pos = lax.broadcasted_iota(jnp.int32, (row_count, key_count), 1)
    scores = jnp.where(query_pos >= key_pos, scores, -jnp.inf)
    row_max = jnp.max(scores, axis=-1, keepdims=True)
    exp_scores = jnp.exp(scores - row_max)
    weights = (exp_scores / jnp.sum(exp_scores, axis=-1, keepdims=True)).astype(jnp.bfloat16)
    mixed_out = jnp.einsum(
        "kgqp,pkd->qkgd", weights, value_tiles, preferred_element_type=jnp.float32
    )
    return mixed_out.reshape(row_count, key_heads * group_width * HEAD_SIZE).astype(jnp.bfloat16)


def attend_all(query_part, key_part, value_part, query_start):
    return attend_rows(query_part, key_part, value_part, query_start)


def local(
    queries, key_rows, value_entries, features, router_score, expert_index, slot_index, expert_grad
):
    key_all, value_all = (
        lax.all_gather(key_rows, "seq", axis=1, tiled=True),
        lax.all_gather(value_entries, "seq", axis=1, tiled=True),
    )
    offset = lax.axis_index("seq") * queries.shape[1]
    attention = jax.vmap(
        lambda query_one, key_one, value_one: attend_all(query_one, key_one, value_one, offset)
    )(queries, key_all, value_all)
    expert_count = lax.axis_size("expert")
    capacity = expert_grad.shape[0] // expert_count
    feature_width = features.shape[1]
    token_count = features.shape[0]
    returned = lax.all_to_all(
        expert_grad.reshape(expert_count, capacity, feature_width),
        "expert",
        split_axis=0,
        concat_axis=0,
        tiled=True,
    )
    returned = returned.reshape(expert_count * capacity, feature_width)
    target = expert_index // EXP_DEV
    slot_cell = target * capacity + slot_index
    cell_grid = lax.broadcasted_iota(jnp.int32, (token_count, expert_count * capacity), 1)
    picker = (slot_cell[:, None] == cell_grid).astype(jnp.bfloat16)
    routed = jnp.dot(picker, returned, preferred_element_type=jnp.float32)
    gate_value = jax.nn.sigmoid(router_score)
    input_grad = (gate_value[:, None] * routed).astype(jnp.bfloat16)
    feature_wide = features.astype(jnp.float32)
    inner_sum = jnp.sum(routed * feature_wide, axis=1)
    score_grad = inner_sum * gate_value * (1.0 - gate_value)
    experts_all = EXP_DEV * expert_count
    column_grid = lax.broadcasted_iota(jnp.int32, (token_count, experts_all), 1)
    weighted = jnp.where(
        expert_index[:, None] == column_grid, score_grad[:, None], jnp.zeros((), jnp.float32)
    )
    per_expert = lax.psum_scatter(
        jnp.dot(weighted.T, feature_wide, precision=lax.Precision.HIGHEST),
        "expert",
        scatter_dimension=0,
        tiled=True,
    )
    router_grad = lax.psum_scatter(per_expert, ("dp", "seq"), scatter_dimension=1, tiled=True)
    return (attention, input_grad, score_grad, router_grad)


def solution(mesh):
    placed = (
        P(("dp", "expert"), "seq", None),
        P(("dp", "expert"), "seq", None),
        P(("dp", "expert"), "seq", None),
        P(("dp", "seq", "expert"), None),
        P(("dp", "seq", "expert")),
        P(("dp", "seq", "expert")),
        P(("dp", "seq", "expert")),
        P(("dp", "seq", "expert"), None),
    )
    return jax.shard_map(
        local,
        mesh=mesh,
        in_specs=placed,
        out_specs=(
            P(("dp", "expert"), "seq", None),
            P(("dp", "seq", "expert"), None),
            P(("dp", "seq", "expert")),
            P("expert", ("dp", "seq")),
        ),
        check_vma=False,
    )
```

profile of v0, /device:TPU:0, one launch (start us, length us, event | category | flops | bytes accessed | tf_op | source)
XLA Modules:
  0.0 108.8 jit_solution(13287607287325676137)
XLA Ops:
  7.2 0.0 copy-start.2
  7.2 0.0 copy-start.4
  7.2 0.0 copy-start.3
  7.2 2.2 %reshape.69 = bf16[4,36,2560]{2,1,0:T(8,128)(2,1)} reshape(bf16[144,2560]{1,0:T(8,128)(2,1)} %param.15) | data formatting | bytes 1474560 | tf_op jit(solution)/shard_map/reshape | solution.py:54
  9.4 0.0 copy-start.6
  9.4 0.0 copy-start.8
  9.4 6.5 %all-to-all-start = ((bf16[4,36,2560]{2,1,0:T(8,128)(2,1)}), bf16[4,36,2560]{2,1,0:T(8,128)(2,1)S(1)}, u32[]{:S(2)}, u32[]{:S(2)}) async-start(bf16[4,36,2560]{2,1,0:T(8,128)(2,1)} %reshape.69), calls=%async_computation | async-start | bytes 1638400 | tf_op jit(solution)/shard_map/all_to_all | solution.py:53
  15.9 0.0 reduce-scatter.5.cloned.1.call-start
  15.9 0.0 copy-done.2
  15.9 1.1 copy.24
  17.0 0.0 copy-done.4
  17.0 0.1 copy.23
  17.1 0.0 copy-done.3
  17.1 5.6 %all_gather.7 = bf16[1,256,512]{2,1,0:T(8,128)(2,1)S(1)} all-gather(bf16[1,128,512]{2,1,0:T(8,128)(2,1)S(1)} %copy-done.3), channel_id=1, replica_groups=mesh['dp'=4,'seq'=2,'expert'=4] {'seq'}, dimensions={1}, use_global_device_ids=true | all-gather | bytes 393216 | tf_op jit(solution)/shard_map/all_gather | solution.py:43
  22.8 0.8 copy.27
  23.6 5.7 %all_gather.6 = bf16[1,256,512]{1,2,0:T(8,128)(2,1)S(1)} all-gather(bf16[1,128,512]{1,2,0:T(8,128)(2,1)S(1)} %copy.23), channel_id=1, replica_groups=mesh['dp'=4,'seq'=2,'expert'=4] {'seq'}, dimensions={1}, use_global_device_ids=true | all-gather | bytes 393216 | tf_op jit(solution)/shard_map/all_gather | solution.py:42
  29.3 0.0 copy-done.6
  29.3 0.0 copy-done.8
  29.3 1.7 %fusion.1 = (f32[4,5,128]{2,1,0:T(8,128)S(1)}, f32[4,256,128,5]{2,1,3,0:T(8,128)S(1)}) fusion(pred[128,256]{0,1:T(8,128)(4,1)S(1)} %iota_compare_fusion.1, bf16[256,4,128,1]{0,2,3,1:T(8,128)(2,1)S(1)} %bitcast.43, bf16[128,4,5,128]{0,3,2,1:T(8,128)(2,1)} %bitcast.42), kind=kOutput, calls=%fused_computation.4 | convolution fusion | flops 169735680 | bytes 3581952 | tf_op jit(solution)/shard_map/vmap(qkgd,pkd->kgqp)/dot_general | solution.py:19
  31.0 0.0 copy-start.7
  31.0 5.7 %all-to-all-done = bf16[4,36,2560]{2,1,0:T(8,128)(2,1)S(1)} async-done(((bf16[4,36,2560]{2,1,0:T(8,128)(2,1)}), bf16[4,36,2560]{2,1,0:T(8,128)(2,1)S(1)}, u32[]{:S(2)}, u32[]{:S(2)}) %all-to-all-start) | async-done | bytes 737312 | tf_op jit(solution)/shard_map/all_to_all | solution.py:53
  36.7 1.0 reshape.70
  37.8 0.0 copy-start.1
  37.8 2.8 %multiply_reduce_fusion = (f32[128]{0:T(128)S(1)}, f32[128,2560]{1,0:T(8,128)}) fusion(bf16[128,2560]{1,0:T(8,128)(2,1)} %param.11, bf16[144,2560]{1,0:T(8,128)(2,1)} %reshape.70, s32[128]{0:T(128)S(1)} %multiply_add_fusion), kind=kOutput, calls=%fused_computation.7 | convolution fusion | flops 95373184 | bytes 2704384 | tf_op jit(solution)/shard_map/dot_general | solution.py:65
  40.6 0.0 copy-done.7
  40.6 0.0 copy-start.5
  40.6 0.0 copy-done.1
  40.6 1.2 %fusion.5 = f32[32,2560]{1,0:T(8,128)} fusion(bf16[128,2560]{1,0:T(8,128)(2,1)S(1)} %copy-done.1, f32[128]{0:T(128)S(1)} %get-tuple-element.16, s32[128]{0:T(128)S(1)} %copy-done.6), kind=kOutput, calls=%fused_computation.13 | convolution fusion | flops 125837312 | bytes 984064 | tf_op jit(solution)/shard_map/dot_general | solution.py:77
  41.9 0.0 reduce-scatter.5.cloned.1.call-update
  41.9 0.0 reduce-scatter.7.cloned.1.call-start
  41.9 0.5 fusion
  42.5 1.8 %convolution_convert_fusion = bf16[4,5,128,128]{2,3,1,0:T(8,128)(2,1)S(1)} fusion(bf16[256,4,128,1]{0,2,3,1:T(8,128)(2,1)} %bitcast.45, f32[4,256,128,5]{2,1,3,0:T(8,128)S(1)} %get-tuple-element.19, f32[4,5,128]{2,1,0:T(8,128)S(1)} %fusion, f32[4,5,128]{2,1,0:T(8,128)S(1)} %get-tuple-element.18, pred[128,256]{0,1:T(8,128)(4,1)S(1)} %iota_compare_fusion.1), kind=kOutput, calls=%fused_computation.5 | convolution fusion | flops 171376640 | bytes 3592192 | tf_op jit(solution)/shard_map/vmap(kgqp,pkd->qkgd)/dot_general | solution.py:28
  44.3 0.0 copy-done.5
  44.3 0.0 copy-start
  44.3 1.1 copy.29
  45.4 16.2 %reduce-scatter.5.cloned.1.call-done = f32[8,2560]{1,0:T(8,128)} async-done(((f32[32,2560]{1,0:T(8,128)}), f32[8,2560]{1,0:T(8,128)}) %reduce-scatter.5.cloned.1.call-update) | async-done | bytes 81936 | tf_op jit(solution)/shard_map/reduce_scatter | solution.py:76
  61.6 2.4 %copy.36 = f32[8,2560]{0,1:T(8,128)} copy(f32[8,2560]{1,0:T(8,128)} %reduce-scatter.5.cloned.1.call-done) | data formatting | bytes 163840
  64.0 0.0 reduce-scatter.7.cloned.1.call-update
  64.0 0.0 copy-done
  64.0 1.0 multiply_convert_fusion
  65.0 35.3 %reduce-scatter.7.cloned.1.call-done = f32[320,8]{1,0:T(8,128)} async-done(((f32[2560,8]{1,0:T(8,128)}), f32[320,8]{1,0:T(8,128)}) %reduce-scatter.7.cloned.1.call-update) | async-done | bytes 10256
  100.4 1.6 %copy.37 = f32[8,320]{1,0:T(8,128)} copy(f32[8,320]{0,1:T(8,128)} %bitcast.46) | data formatting | bytes 20480
  (4 shorter events, 0.0 us)
Async XLA Ops:
  7.2 8.8 %copy-start.2 = (bf16[1,128,2560]{2,1,0:T(8,128)(2,1)S(1)}, bf16[1,128,2560]{2,1,0:T(8,128)(2,1)}, u32[]{:S(2)}) copy-start(bf16[1,128,2560]{2,1,0:T(8,128)(2,1)} %param.8) | copy-start | bytes 1966084
  7.2 9.8 %copy-start.4 = (bf16[1,128,512]{2,1,0:T(8,128)(2,1)S(1)}, bf16[1,128,512]{2,1,0:T(8,128)(2,1)}, u32[]{:S(2)}) copy-start(bf16[1,128,512]{2,1,0:T(8,128)(2,1)} %param.9) | copy-start | bytes 393220
  7.2 9.9 %copy-start.3 = (bf16[1,128,512]{2,1,0:T(8,128)(2,1)S(1)}, bf16[1,128,512]{2,1,0:T(8,128)(2,1)}, u32[]{:S(2)}) copy-start(bf16[1,128,512]{2,1,0:T(8,128)(2,1)} %param.10) | copy-start | bytes 393220
  9.4 19.8 %copy-start.6 = (s32[128]{0:T(128)S(1)}, s32[128]{0:T(128)}, u32[]{:S(2)}) copy-start(s32[128]{0:T(128)} %param.13) | copy-start | bytes 1540
  9.4 19.8 %copy-start.8 = (s32[128]{0:T(128)S(1)}, s32[128]{0:T(128)}, u32[]{:S(2)}) copy-start(s32[128]{0:T(128)} %param.14) | copy-start | bytes 1540
  9.4 27.3 %all-to-all-start = ((bf16[4,36,2560]{2,1,0:T(8,128)(2,1)}), bf16[4,36,2560]{2,1,0:T(8,128)(2,1)S(1)}, u32[]{:S(2)}, u32[]{:S(2)}) async-start(bf16[4,36,2560]{2,1,0:T(8,128)(2,1)} %reshape.69), calls=%async_computation | async-start | bytes 1638400 | tf_op jit(solution)/shard_map/all_to_all | solution.py:53
  15.9 45.7 %reduce-scatter.5.cloned.1.call-start = ((), (), s32[]{:S(2)}) async-start(), calls=%async_computation.3 | async-start | bytes 409600 | tf_op jit(solution)/shard_map/reduce_scatter | solution.py:76
  31.0 9.6 %copy-start.7 = (f32[128]{0:T(128)S(1)}, f32[128]{0:T(128)}, u32[]{:S(2)}) copy-start(f32[128]{0:T(128)} %param.12) | copy-start | bytes 1540
  37.8 2.9 %copy-start.1 = (bf16[128,2560]{1,0:T(8,128)(2,1)S(1)}, bf16[128,2560]{1,0:T(8,128)(2,1)}, u32[]{:S(2)}) copy-start(bf16[128,2560]{1,0:T(8,128)(2,1)} %param.11) | copy-start | bytes 1966084
  40.6 3.7 %copy-start.5 = (f32[128]{0:T(128)}, f32[128]{0:T(128)S(1)}, u32[]{:S(2)}) copy-start(f32[128]{0:T(128)S(1)} %get-tuple-element.16) | copy-start | bytes 1540
  41.9 58.5 %reduce-scatter.7.cloned.1.call-start = ((), (), s32[]{:S(2)}) async-start(), calls=%async_computation.4 | async-start | bytes 1474560
  44.3 19.7 %copy-start = (f32[128,2560]{1,0:T(8,128)S(1)}, f32[128,2560]{1,0:T(8,128)}, u32[]{:S(2)}) copy-start(f32[128,2560]{1,0:T(8,128)} %get-tuple-element.21) | copy-start | bytes 3932164
Sparse Core Ops, SparseCore 0:
  42.0 19.5 reduce-scatter.4
  64.9 35.4 reduce-scatter.6
where the time goes:
time: 109 us
  waiting for transfers between devices  57.3 us (53%)
  between operations  14.2 us (13%)
  blocking collectives  11.3 us (10%)
  local copies, waits for them, and re-layouts  10.4 us (10%)
  matrix products  7.54 us (7%)
  starting transfers between devices  6.52 us (6%)
  other arithmetic  1.57 us (1%)
    unnamed x3, waiting for transfers between devices  35.4 us
    reduce_scatter x1, waiting for transfers between devices, local(): lax.psum_scatter(jnp.dot(weighted.T, feature_wide, precision=lax.Precisio...  16.2 us
    all_to_all x1, starting transfers between devices, local(): lax.all_to_all(expert_grad.reshape(expert_count, capacity, feature_width)...  6.48 us
    unnamed x23, local copies, waits for them, and re-layouts  6.3 us
    all_to_all x1, waiting for transfers between devices, local(): lax.all_to_all(expert_grad.reshape(expert_count, capacity, feature_width)...  5.73 us
    all_gather x1, blocking collectives, local(): lax.all_gather(key_rows, 'seq', axis=1, tiled=True)  5.65 us
    all_gather x1, blocking collectives, local(): lax.all_gather(value_entries, 'seq', axis=1, tiled=True)  5.64 us
    dot_general x1, matrix products, local(): routed = jnp.dot(picker, returned, preferred_element_type=jnp.float32)  2.82 us
  transfers between devices with their start and end apart: 3, of which 3 were waited for; matrix products, arithmetic and copies ran while one was open for 7% of the time, Pallas kernels for 0%

commit v1 on v0

--- a/solution.py
+++ b/solution.py
@@ -40,7 +40,9 @@
 ):
     key_all, value_all = (
         lax.all_gather(key_rows, "seq", axis=1, tiled=True),
-        lax.all_gather(value_entries, "seq", axis=1, tiled=True),
+        jnp.concatenate(
+            lax.all_to_all(jnp.stack([value_entries] * lax.axis_size("seq")), "seq", 0, 0), axis=1
+        ),
     )
     offset = lax.axis_index("seq") * queries.shape[1]
     attention = jax.vmap(

time: 109 us -> 114 us (1.046)
  blocking collectives: 11.3 us -> 5.68 us
  waiting for transfers between devices: 57.3 us -> 61.9 us
  starting transfers between devices: 6.52 us -> 10.5 us
    all_to_all x1, waiting for transfers between devices: 5.73 us -> 11.5 us  [local(): lax.all_to_all(expert_grad.reshape(expert_count, capacity, feature_width)...]
    all_gather x1 -> x0, blocking collectives: 5.64 us -> none  [local(): lax.all_gather(value_entries, 'seq', axis=1, tiled=True)]
    all_to_all x0 -> x1, starting transfers between devices: none -> 4.11 us  [local(): lax.all_to_all(jnp.stack([value_entries] * lax.axis_size('seq')), 'seq',...]
    another operation x0 -> x1, local copies, waits for them, and re-layouts: none -> 1.72 us
    reduce_scatter x1, waiting for transfers between devices: 16.2 us -> 15 us  [local(): lax.psum_scatter(jnp.dot(weighted.T, feature_wide, precision=lax.Precisio...]
  transfers between devices with their start and end apart: 3 -> 4, of which waited for: 3 -> 3; matrix products, arithmetic and copies ran while one was open for 7% -> 13% of each run, Pallas kernels for 0% -> 0%
where the time goes in v1:
time: 114 us; the launch traced here: 113 us
  waiting for transfers between devices  61.9 us (54%)
  between operations  14.2 us (12%)
  local copies, waits for them, and re-layouts  11.3 us (10%)
  starting transfers between devices  10.5 us (9%)
  matrix products  7.51 us (7%)
  blocking collectives  5.68 us (5%)
  other arithmetic  2.29 us (2%)
    unnamed x3, waiting for transfers between devices  35.4 us
    reduce_scatter x1, waiting for transfers between devices, local(): lax.psum_scatter(jnp.dot(weighted.T, feature_wide, precision=lax.Precisio...  15 us
    all_to_all x1, waiting for transfers between devices, local(): lax.all_to_all(expert_grad.reshape(expert_count, capacity, feature_width)...  11.5 us
    all_to_all x1, starting transfers between devices, local(): lax.all_to_all(expert_grad.reshape(expert_count, capacity, feature_width)...  6.35 us
    unnamed x23, local copies, waits for them, and re-layouts  6.3 us
    all_gather x1, blocking collectives, local(): lax.all_gather(key_rows, 'seq', axis=1, tiled=True)  5.68 us
    all_to_all x1, starting transfers between devices, local(): lax.all_to_all(jnp.stack([value_entries] * lax.axis_size('seq')), 'seq',...  4.11 us
    dot_general x1, matrix products, local(): routed = jnp.dot(picker, returned, preferred_element_type=jnp.float32)  2.83 us
  transfers between devices with their start and end apart: 4, of which 3 were waited for; matrix products, arithmetic and copies ran while one was open for 13% of the time, Pallas kernels for 0%

profile of v1, /device:TPU:0, one launch (start us, length us, event | category | flops | bytes accessed | tf_op | source)
XLA Modules:
  0.0 113.3 jit_solution(9826471247062040278)
XLA Ops:
  7.2 0.0 copy-start.2
  7.2 0.0 copy-start.4
  7.2 0.0 copy-start.3
  7.2 0.0 copy-start.6
  7.2 0.0 copy-start.8
  7.2 2.2 %reshape.68 = bf16[4,36,2560]{2,1,0:T(8,128)(2,1)} reshape(bf16[144,2560]{1,0:T(8,128)(2,1)} %param.15) | data formatting | bytes 1474560 | tf_op jit(solution)/shard_map/reshape | solution.py:56
  9.4 6.3 %all-to-all-start.1 = ((bf16[4,36,2560]{2,1,0:T(8,128)(2,1)}), bf16[4,36,2560]{2,1,0:T(8,128)(2,1)S(1)}, u32[]{:S(2)}, u32[]{:S(2)}) async-start(bf16[4,36,2560]{2,1,0:T(8,128)(2,1)} %reshape.68), calls=%async_computation.1 | async-start | bytes 1638400 | tf_op jit(solution)/shard_map/all_to_all | solution.py:55
  15.8 0.0 copy-done.2
  15.8 1.1 copy.25
  16.9 0.0 copy-done.4
  16.9 0.1 copy.24
  17.0 5.7 %all_gather.3 = bf16[1,256,512]{1,2,0:T(8,128)(2,1)S(1)} all-gather(bf16[1,128,512]{1,2,0:T(8,128)(2,1)S(1)} %copy.24), channel_id=1, replica_groups=mesh['dp'=4,'seq'=2,'expert'=4] {'seq'}, dimensions={1}, use_global_device_ids=true | all-gather | bytes 393216 | tf_op jit(solution)/shard_map/all_gather | solution.py:42
  22.7 0.0 copy-done.3
  22.7 0.7 pad_maximum_fusion
  23.4 0.0 copy-done.6
  23.4 0.0 copy-done.8
  23.5 1.6 %fusion.1 = (f32[4,5,128]{2,1,0:T(8,128)S(1)}, f32[4,256,128,5]{2,1,3,0:T(8,128)S(1)}) fusion(pred[128,256]{0,1:T(8,128)(4,1)S(1)} %iota_compare_fusion.1, bf16[256,4,128,1]{0,2,3,1:T(8,128)(2,1)S(1)} %bitcast.39, bf16[128,4,5,128]{0,3,2,1:T(8,128)(2,1)} %bitcast.38), kind=kOutput, calls=%fused_computation.4 | convolution fusion | flops 169735680 | bytes 3581952 | tf_op jit(solution)/shard_map/vmap(qkgd,pkd->kgqp)/dot_general | solution.py:19
  25.1 0.0 copy-start.7
  25.1 11.5 %all-to-all-done.1 = bf16[4,36,2560]{2,1,0:T(8,128)(2,1)S(1)} async-done(((bf16[4,36,2560]{2,1,0:T(8,128)(2,1)}), bf16[4,36,2560]{2,1,0:T(8,128)(2,1)S(1)}, u32[]{:S(2)}, u32[]{:S(2)}) %all-to-all-start.1) | async-done | bytes 737312 | tf_op jit(solution)/shard_map/all_to_all | solution.py:55
  36.6 4.1 %all-to-all-start = ((bf16[2,1,128,512]{3,2,1,0:T(8,128)(2,1)}), bf16[2,1,128,512]{3,2,1,0:T(8,128)(2,1)}, u32[]{:S(2)}, u32[]{:S(2)}) async-start(bf16[2,1,128,512]{3,2,1,0:T(8,128)(2,1)} %pad_maximum_fusion), calls=%async_computation | async-start | bytes 524288 | tf_op jit(solution)/shard_map/all_to_all | solution.py:44
  40.7 0.0 reduce-scatter.5.cloned.1.call-start
  40.8 1.0 reshape.69
  41.8 0.0 copy-start.1
  41.8 2.8 %multiply_reduce_fusion = (f32[128]{0:T(128)S(1)}, f32[128,2560]{1,0:T(8,128)}) fusion(bf16[128,2560]{1,0:T(8,128)(2,1)} %param.11, bf16[144,2560]{1,0:T(8,128)(2,1)} %reshape.69, s32[128]{0:T(128)S(1)} %multiply_add_fusion), kind=kOutput, calls=%fused_computation.7 | convolution fusion | flops 95373184 | bytes 2704384 | tf_op jit(solution)/shard_map/dot_general | solution.py:67
  44.6 0.0 copy-done.7
  44.6 0.0 copy-start.5
  44.6 0.0 copy-done.1
  44.7 1.2 %fusion.6 = f32[32,2560]{1,0:T(8,128)} fusion(bf16[128,2560]{1,0:T(8,128)(2,1)S(1)} %copy-done.1, f32[128]{0:T(128)S(1)} %get-tuple-element.16, s32[128]{0:T(128)S(1)} %copy-done.6), kind=kOutput, calls=%fused_computation.15 | convolution fusion | flops 125837312 | bytes 984064 | tf_op jit(solution)/shard_map/dot_general | solution.py:79
  45.9 0.0 reduce-scatter.5.cloned.1.call-update
  45.9 0.0 reduce-scatter.7.cloned.1.call-start
  46.0 0.5 fusion
  46.5 0.0 all-to-all-done
  46.5 1.7 %reshape.72 = bf16[256,4,128]{2,1,0:T(4,128)(2,1)} reshape(bf16[2,1,128,512]{3,2,1,0:T(8,128)(2,1)} %all-to-all-done) | data formatting | bytes 524288 | tf_op jit(solution)/shard_map/reshape.10
  48.2 1.8 %convolution_convert_fusion = bf16[4,128,5,128]{3,1,2,0:T(8,128)(2,1)S(1)} fusion(f32[4,256,128,5]{2,1,3,0:T(8,128)S(1)} %get-tuple-element.19, f32[4,5,128]{2,1,0:T(8,128)S(1)} %fusion, f32[4,5,128]{2,1,0:T(8,128)S(1)} %get-tuple-element.18, pred[128,256]{0,1:T(8,128)(4,1)S(1)} %iota_compare_fusion.1, bf16[256,4,128,1]{2,1,0,3:T(4,128)(2,1)} %bitcast.41), kind=kOutput, calls=%fused_computation.5 | convolution fusion | flops 171376640 | bytes 3592192 | tf_op jit(solution)/shard_map/vmap(kgqp,pkd->qkgd)/dot_general | solution.py:28
  50.0 0.0 copy-done.5
  50.1 0.0 copy-start
  50.1 1.1 copy.29
  51.2 15.0 %reduce-scatter.5.cloned.1.call-done = f32[8,2560]{1,0:T(8,128)} async-done(((f32[32,2560]{1,0:T(8,128)}), f32[8,2560]{1,0:T(8,128)}) %reduce-scatter.5.cloned.1.call-update) | async-done | bytes 81936 | tf_op jit(solution)/shard_map/reduce_scatter | solution.py:78
  66.1 2.4 %copy.39 = f32[8,2560]{0,1:T(8,128)} copy(f32[8,2560]{1,0:T(8,128)} %reduce-scatter.5.cloned.1.call-done) | data formatting | bytes 163840
  68.5 0.0 reduce-scatter.7.cloned.1.call-update
  68.5 0.0 copy-done
  68.5 1.0 multiply_convert_fusion
  69.5 35.4 %reduce-scatter.7.cloned.1.call-done = f32[320,8]{1,0:T(8,128)} async-done(((f32[2560,8]{1,0:T(8,128)}), f32[320,8]{1,0:T(8,128)}) %reduce-scatter.7.cloned.1.call-update) | async-done | bytes 10256
  104.9 1.6 %copy.40 = f32[8,320]{1,0:T(8,128)} copy(f32[8,320]{0,1:T(8,128)} %bitcast.42) | data formatting | bytes 20480
  (4 shorter events, 0.0 us)
Async XLA Ops:
  7.2 8.6 %copy-start.2 = (bf16[1,128,2560]{2,1,0:T(8,128)(2,1)S(1)}, bf16[1,128,2560]{2,1,0:T(8,128)(2,1)}, u32[]{:S(2)}) copy-start(bf16[1,128,2560]{2,1,0:T(8,128)(2,1)} %param.8) | copy-start | bytes 1966084
  7.2 9.7 %copy-start.4 = (bf16[1,128,512]{2,1,0:T(8,128)(2,1)S(1)}, bf16[1,128,512]{2,1,0:T(8,128)(2,1)}, u32[]{:S(2)}) copy-start(bf16[1,128,512]{2,1,0:T(8,128)(2,1)} %param.9) | copy-start | bytes 393220
  7.2 15.5 %copy-start.3 = (bf16[1,128,512]{2,1,0:T(8,128)(2,1)S(1)}, bf16[1,128,512]{2,1,0:T(8,128)(2,1)}, u32[]{:S(2)}) copy-start(bf16[1,128,512]{2,1,0:T(8,128)(2,1)} %param.10) | copy-start | bytes 393220
  7.2 16.2 %copy-start.6 = (s32[128]{0:T(128)S(1)}, s32[128]{0:T(128)}, u32[]{:S(2)}) copy-start(s32[128]{0:T(128)} %param.13) | copy-start | bytes 1540
  7.2 16.2 %copy-start.8 = (s32[128]{0:T(128)S(1)}, s32[128]{0:T(128)}, u32[]{:S(2)}) copy-start(s32[128]{0:T(128)} %param.14) | copy-start | bytes 1540
  9.4 27.2 %all-to-all-start.1 = ((bf16[4,36,2560]{2,1,0:T(8,128)(2,1)}), bf16[4,36,2560]{2,1,0:T(8,128)(2,1)S(1)}, u32[]{:S(2)}, u32[]{:S(2)}) async-start(bf16[4,36,2560]{2,1,0:T(8,128)(2,1)} %reshape.68), calls=%async_computation.1 | async-start | bytes 1638400 | tf_op jit(solution)/shard_map/all_to_all | solution.py:55
  25.1 19.5 %copy-start.7 = (f32[128]{0:T(128)S(1)}, f32[128]{0:T(128)}, u32[]{:S(2)}) copy-start(f32[128]{0:T(128)} %param.12) | copy-start | bytes 1540
  36.6 9.9 %all-to-all-start = ((bf16[2,1,128,512]{3,2,1,0:T(8,128)(2,1)}), bf16[2,1,128,512]{3,2,1,0:T(8,128)(2,1)}, u32[]{:S(2)}, u32[]{:S(2)}) async-start(bf16[2,1,128,512]{3,2,1,0:T(8,128)(2,1)} %pad_maximum_fusion), calls=%async_computation | async-start | bytes 524288 | tf_op jit(solution)/shard_map/all_to_all | solution.py:44
  40.7 25.4 %reduce-scatter.5.cloned.1.call-start = ((), (), s32[]{:S(2)}) async-start(), calls=%async_computation.4 | async-start | bytes 409600 | tf_op jit(solution)/shard_map/reduce_scatter | solution.py:78
  41.8 2.9 %copy-start.1 = (bf16[128,2560]{1,0:T(8,128)(2,1)S(1)}, bf16[128,2560]{1,0:T(8,128)(2,1)}, u32[]{:S(2)}) copy-start(bf16[128,2560]{1,0:T(8,128)(2,1)} %param.11) | copy-start | bytes 1966084
  44.6 5.4 %copy-start.5 = (f32[128]{0:T(128)}, f32[128]{0:T(128)S(1)}, u32[]{:S(2)}) copy-start(f32[128]{0:T(128)S(1)} %get-tuple-element.16) | copy-start | bytes 1540
  45.9 59.0 %reduce-scatter.7.cloned.1.call-start = ((), (), s32[]{:S(2)}) async-start(), calls=%async_computation.5 | async-start | bytes 1474560
  50.1 18.5 %copy-start = (f32[128,2560]{1,0:T(8,128)S(1)}, f32[128,2560]{1,0:T(8,128)}, u32[]{:S(2)}) copy-start(f32[128,2560]{1,0:T(8,128)} %get-tuple-element.21) | copy-start | bytes 3932164
Sparse Core Ops, SparseCore 0:
  46.0 20.0 reduce-scatter.4
  69.4 35.4 reduce-scatter.6
